TPU v7x, 256 devices: a 2x2x32 block of a 4x8x32 slice. The times are simulated.
256 devices in a mesh: parts: 4 (over y, x), dp: 64 (over z, core).
Axes of the slice: x: 2, y: 2, z: 32, core: 2. Of those that a mesh axis runs over, the one named last changes fastest.
The devices are a block of a 4x8x32 slice.
Arguments:
- activations: bfloat16 [65536, 14336], P(('parts', 'dp')), parts along dimension 0, may hold values from -6 to 6
- out_grads: bfloat16 [65536, 4096], P(('parts', 'dp')), parts along dimension 0, may hold values from -6 to 6
- lengths: int32 [256, 4], P(('parts', 'dp')), parts along dimension 0, may hold values from 1 to 128, 256 in all within a row
- proj_in: bfloat16 [14336, 64], replicated, may hold values from -0.046875 to 0.046875
- proj_out: bfloat16 [4096, 64], replicated, may hold values from -0.09375 to 0.09375
- queries: bfloat16 [8192, 4096], P(('parts', 'dp')), parts along dimension 0, may hold values from -0.01171875 to 0.01171875
Outputs:
- scores: bfloat16 [1024, 2048], P(('parts', 'dp')), parts along dimension 0
There are 4 independent parts, one for each index of `parts`. A program takes and returns all parts, laid end to end along the dimension named above; an argument that names none is the same for every part. Nothing has to cross between parts.
Inputs may be any that keep to these rules, and one draw needn't show every extreme that they name: Each row of lengths sums to 256, and one entry of each row equals 128.
All inputs are finite; a program needn't handle non-finite values.
Results may differ from a plain program's by a relative error of at most 0.0065.
Values may be sent and summed in bfloat16 or wider, within the bound.
A program may use at most 128 MiB of HBM per device.

v0:
```python
import jax
import jax.numpy as jnp
from jax import lax
from jax.sharding import PartitionSpec as P


def local(activations, out_grads, lengths, proj_in, proj_out, queries):
    tok_count = activations.shape[0]
    rank_size = proj_in.shape[1]
    proj_acts = jnp.dot(activations, proj_in, preferred_element_type=jnp.float32).astype(
        jnp.bfloat16
    )
    proj_grads = jnp.dot(out_grads, proj_out, preferred_element_type=jnp.float32).astype(
        jnp.bfloat16
    )
    counts = lengths[0]
    examples = counts.shape[0]
    position = jnp.arange(tok_count, dtype=jnp.int32)
    tok_ends = [counts[0]]
    for e in range(1, examples):
        tok_ends.append(tok_ends[-1] + counts[e])
    owner = sum(((position >= end).astype(jnp.int32) for end in tok_ends[:-1]))
    member = (owner[:, None] == jnp.arange(examples)[None, :]).astype(jnp.bfloat16)
    masked = (member[:, :, None] * proj_acts[:, None, :]).reshape(tok_count, examples * rank_size)
    summed = lax.dot_general(
        proj_grads, masked, (((0,), (0,)), ((), ())), preferred_element_type=jnp.float32
    )
    example_grads = (
        summed.reshape(rank_size, examples, rank_size)
        .transpose(1, 0, 2)
        .reshape(examples, rank_size * rank_size)
        .astype(jnp.bfloat16)
    )
    contract = (((1,), (1,)), ((), ()))
    scores = lax.dot_general(
        lax.all_gather(example_grads, "dp", axis=0, tiled=True),
        queries,
        contract,
        preferred_element_type=jnp.float32,
    ).astype(jnp.bfloat16)
    return lax.all_to_all(scores, "dp", split_axis=0, concat_axis=1, tiled=True)


def solution(mesh):
    in_specs = (
        P(("parts", "dp"), None),
        P(("parts", "dp"), None),
        P(("parts", "dp"), None),
        P(),
        P(),
        P(("parts", "dp"), None),
    )
    out_specs = P(("parts", "dp"), None)
    return jax.shard_map(local, mesh=mesh, in_specs=in_specs, out_specs=out_specs, check_vma=False)
```

profile of v0, /device:TPU:37, one launch (start us, length us, event | category | flops | bytes accessed | tf_op | source)
XLA Modules:
  0.0 216.6 jit_solution(11846224290307808529)
XLA Ops:
  6.5 0.0 copy-start
  6.6 0.0 all-gather.3.cloned.1.call-start
  6.6 1.4 fusion.9
  9.9 0.7 fusion.8
  10.6 0.0 copy-start.1
  10.6 6.0 %convolution_convert_fusion.1 = bf16[256,64]{0,1:T(8,128)(2,1)S(1)} fusion(bf16[256,14336]{1,0:T(8,128)(2,1)} %param.6, bf16[14336,64]{0,1:T(8,128)(2,1)} %param.9), kind=kOutput, calls=%fused_computation.2 | convolution fusion | flops 469778432 | bytes 9207808 | tf_op jit(solution)/shard_map/dot_general | solution.py:10
  16.6 0.0 copy-done
  16.6 0.0 copy-done.1
  16.6 1.0 fusion
  17.6 0.7 reshape.52
  18.3 0.1 all-gather.3.cloned.1.call-update
  18.4 0.0 copy-start.2
  18.4 145.2 %all-gather.3.cloned.1.call-done = bf16[64,4,4096]{2,1,0:T(4,128)(2,1)} async-done(((bf16[1,4,4096]{2,1,0:T(4,128)(2,1)}), bf16[64,4,4096]{2,1,0:T(4,128)(2,1)}) %all-gather.3.cloned.1.call-update) | async-done | bytes 2097168 | tf_op jit(solution)/shard_map/all_gather | solution.py:36
  163.6 4.0 %reshape.53 = bf16[256,4096]{1,0:T(8,128)(2,1)} reshape(bf16[64,4,4096]{2,1,0:T(4,128)(2,1)} %all-gather.3.cloned.1.call-done) | data formatting | bytes 4194304
  167.6 0.0 copy-done.2
  167.6 2.3 %convolution_convert_fusion.3 = bf16[256,32]{0,1:T(8,128)(2,1)S(1)} fusion(bf16[256,4096]{1,0:T(8,128)(2,1)} %reshape.53, bf16[32,4096]{1,0:T(8,128)(2,1)S(1)} %copy-done.2), kind=kOutput, calls=%fused_computation.5 | convolution fusion | flops 67117056 | bytes 2375680 | tf_op jit(solution)/shard_map/dot_general | solution.py:35
  169.9 0.1 copy.10
  170.0 39.0 %all_to_all.19 = bf16[64,4,32]{2,1,0:T(4,128)(2,1)S(1)} all-to-all(bf16[64,4,32]{2,1,0:T(4,128)(2,1)S(1)} %bitcast.24), channel_id=1, replica_groups=mesh['parts'=4,'dp'=64] {'dp'}, dimensions={0} | all-to-all | bytes 32768 | tf_op jit(solution)/shard_map/all_to_all | solution.py:41
  209.0 0.7 all_to_all.17
  (2 shorter events, 0.0 us)
Async XLA Ops:
  6.5 10.1 %copy-start = (bf16[256,4096]{1,0:T(8,128)(2,1)S(1)}, bf16[256,4096]{1,0:T(8,128)(2,1)}, u32[]{:S(2)}) copy-start(bf16[256,4096]{1,0:T(8,128)(2,1)} %param.7) | copy-start | bytes 6291460
  6.6 157.1 %all-gather.3.cloned.1.call-start = ((), (), s32[]{:S(2)}) async-start(), calls=%async_computation.1 | async-start | bytes 2129920 | tf_op jit(solution)/shard_map/all_gather | solution.py:36
  10.6 6.0 %copy-start.1 = (bf16[4096,64]{0,1:T(8,128)(2,1)S(1)}, bf16[4096,64]{0,1:T(8,128)(2,1)}, u32[]{:S(2)}) copy-start(bf16[4096,64]{0,1:T(8,128)(2,1)} %param.10) | copy-start | bytes 1572868
  18.4 149.2 %copy-start.2 = (bf16[32,4096]{1,0:T(8,128)(2,1)S(1)}, bf16[32,4096]{1,0:T(8,128)(2,1)}, u32[]{:S(2)}) copy-start(bf16[32,4096]{1,0:T(8,128)(2,1)} %param.11) | copy-start | bytes 786436
Sparse Core Ops, SparseCore 0:
  18.5 145.0 all-gather.2
where the time goes:
time: 217 us
  waiting for transfers between devices  145 us (67%)
  blocking collectives  39 us (18%)
  between operations  15.4 us (7%)
  matrix products  9.29 us (4%)
  local copies, waits for them, and re-layouts  7.01 us (3%)
    all_gather x1, waiting for transfers between devices, local(): lax.all_gather(example_grads, 'dp', axis=0, tiled=True)  145 us
    all_to_all x1, blocking collectives, local(): return lax.all_to_all(scores, 'dp', split_axis=0, concat_axis=1, tiled=True)  39 us
    dot_general x1, matrix products, local(): jnp.dot(activations, proj_in, preferred_element_type=jnp.float32)  5.99 us
    unnamed x8, local copies, waits for them, and re-layouts  4.71 us
  transfers between devices with their start and end apart: 1, of which 1 were waited for; matrix products, arithmetic and copies ran while one was open for 0% of the time, Pallas kernels for 0%

commit v1 on v0

--- a/solution.py
+++ b/solution.py
@@ -33,7 +33,9 @@
     )
     contract = (((1,), (1,)), ((), ()))
     scores = lax.dot_general(
-        lax.all_gather(example_grads, "dp", axis=0, tiled=True),
+        jnp.concatenate(
+            lax.all_to_all(jnp.stack([example_grads] * lax.axis_size("dp")), "dp", 0, 0), axis=0
+        ),
         queries,
         contract,
         preferred_element_type=jnp.float32,

time: 217 us -> 283 us (1.30)
  blocking collectives: 39 us -> 263 us
  waiting for transfers between devices: 145 us -> 0 us
  between operations: 15.4 us -> 1.95 us
    all_to_all x0 -> x1, blocking collectives: none -> 232 us  [local(): lax.all_to_all(jnp.stack([example_grads] * lax.axis_size('dp')), 'dp', 0, 0)]
    all_gather x1 -> x0, waiting for transfers between devices: 145 us -> none  [local(): lax.all_gather(example_grads, 'dp', axis=0, tiled=True)]
    all_to_all x1, blocking collectives: 39 us -> 31.7 us  [local(): return lax.all_to_all(scores, 'dp', split_axis=0, concat_axis=1, tiled=True)]
    unnamed x8 -> x6, local copies, waits for them, and re-layouts: 4.71 us -> 0.01 us
    reshape x0 -> x1, local copies, waits for them, and re-layouts: none -> 3.99 us  [local(): jnp.concatenate(lax.all_to_all(jnp.stack([example_grads] * lax.axis_size(...]
  transfers between devices with their start and end apart: 1 -> 0, of which waited for: 1 -> 0; matrix products, arithmetic and copies ran while one was open for 0% -> 0% of each run, Pallas kernels for 0% -> 0%
where the time goes in v1:
time: 283 us
  blocking collectives  263 us (93%)
  matrix products  9.29 us (3%)
  local copies, waits for them, and re-layouts  7.42 us (3%)
    all_to_all x1, blocking collectives, local(): lax.all_to_all(jnp.stack([example_grads] * lax.axis_size('dp')), 'dp', 0, 0)  232 us
    all_to_all x1, blocking collectives, local(): return lax.all_to_all(scores, 'dp', split_axis=0, concat_axis=1, tiled=True)  31.7 us
    dot_general x1, matrix products, local(): jnp.dot(activations, proj_in, preferred_element_type=jnp.float32)  5.99 us

profile of v1, /device:TPU:37, one launch (start us, length us, event | category | flops | bytes accessed | tf_op | source)
XLA Modules:
  0.0 282.5 jit_solution(8835142113678143529)
XLA Ops:
  0.0 0.0 copy-start
  0.0 1.4 fusion.9
  3.3 0.6 fusion.8
  3.9 0.0 copy-start.1
  4.0 6.0 %convolution_convert_fusion.1 = bf16[256,64]{0,1:T(8,128)(2,1)S(1)} fusion(bf16[256,14336]{1,0:T(8,128)(2,1)} %param.6, bf16[14336,64]{0,1:T(8,128)(2,1)} %param.9), kind=kOutput, calls=%fused_computation.2 | convolution fusion | flops 469778432 | bytes 9207808 | tf_op jit(solution)/shard_map/dot_general | solution.py:10
  9.9 0.0 copy-done
  10.0 0.0 copy-done.1
  10.0 1.0 fusion
  11.0 0.1 convert_element_type.56
  11.1 1.0 stack.2
  12.1 231.6 %all_to_all.24 = bf16[64,4,4096]{2,1,0:T(4,128)(2,1)} all-to-all(bf16[64,4,4096]{2,1,0:T(4,128)(2,1)S(1)} %stack.2), channel_id=1, replica_groups=mesh['parts'=4,'dp'=64] {'dp'}, dimensions={0} | all-to-all | bytes 4194304 | tf_op jit(solution)/shard_map/all_to_all | solution.py:37
  243.7 0.0 copy-start.2
  243.7 4.0 %reshape.58 = bf16[256,4096]{1,0:T(8,128)(2,1)} reshape(bf16[64,4,4096]{2,1,0:T(4,128)(2,1)} %all_to_all.24) | data formatting | bytes 4194304 | tf_op jit(solution)/shard_map/reshape | solution.py:36
  247.7 0.0 copy-done.2
  247.7 2.3 convolution_convert_fusion.3
  250.0 0.1 copy.8
  250.1 31.7 %all_to_all.25 = bf16[64,4,32]{2,1,0:T(4,128)(2,1)S(1)} all-to-all(bf16[64,4,32]{2,1,0:T(4,128)(2,1)S(1)} %bitcast.24), channel_id=1, replica_groups=mesh['parts'=4,'dp'=64] {'dp'}, dimensions={0} | all-to-all | bytes 32768 | tf_op jit(solution)/shard_map/all_to_all | solution.py:43
  281.8 0.7 all_to_all.21
  (2 shorter events, 0.0 us)
Async XLA Ops:
  0.0 9.9 %copy-start = (bf16[256,4096]{1,0:T(8,128)(2,1)S(1)}, bf16[256,4096]{1,0:T(8,128)(2,1)}, u32[]{:S(2)}) copy-start(bf16[256,4096]{1,0:T(8,128)(2,1)} %param.7) | copy-start | bytes 6291460
  3.9 6.0 %copy-start.1 = (bf16[4096,64]{0,1:T(8,128)(2,1)S(1)}, bf16[4096,64]{0,1:T(8,128)(2,1)}, u32[]{:S(2)}) copy-start(bf16[4096,64]{0,1:T(8,128)(2,1)} %param.10) | copy-start | bytes 1572868
  243.7 4.0 %copy-start.2 = (bf16[32,4096]{1,0:T(8,128)(2,1)S(1)}, bf16[32,4096]{1,0:T(8,128)(2,1)}, u32[]{:S(2)}) copy-start(bf16[32,4096]{1,0:T(8,128)(2,1)} %param.11) | copy-start | bytes 786436
